TPU v7x, 32 devices: a whole 2x2x4 slice. The times are simulated.
32 devices in a mesh: groups: 2 (over x), ctx: 16 (over z, y, core).
Axes of the slice: x: 2, y: 2, z: 4, core: 2. Of those that a mesh axis runs over, the one named last changes fastest.
Arguments:
- queries: bfloat16 [256, 2048], P(('groups', 'ctx')), parts along dimension 0, may hold values from -200 to 200
- slab_keys: bfloat16 [256, 2048], P(('groups', 'ctx')), parts along dimension 0, may hold values from -6 to 6
- slab_values: bfloat16 [256, 2048], P(('groups', 'ctx')), parts along dimension 0, may hold values from -6 to 6
- cache_keys: bfloat16 [16384, 2048], P(('groups', 'ctx')), parts along dimension 0, may hold values from -12 to 12
- cache_values: bfloat16 [16384, 2048], P(('groups', 'ctx')), parts along dimension 0, may hold values from -6 to 6
- offset: int32 [2], P('groups'), parts along dimension 0, may hold values from 2048 to 8192
- slab_len: int32 [2], P('groups'), parts along dimension 0, may hold values from 64 to 128
Outputs:
- attended: bfloat16 [256, 2048], P(('groups', 'ctx')), parts along dimension 0
There are 2 independent parts, one for each index of `groups`. A program takes and returns all parts, laid end to end along the dimension named above; each array names one. Nothing has to cross between parts.
All inputs are finite; a program needn't handle non-finite values.
Results may differ from a plain program's by a relative error of at most 0.0081.
Values may be sent and summed in bfloat16 or wider, within the bound.
A program may use at most 128 MiB of HBM per device.

v0:
```python
import jax
import jax.numpy as jnp
from jax import lax
from jax.sharding import PartitionSpec as P

DH = 128
KB = 256


very_low = -1e30


def block_state(query_heads, key_blocks, value_blocks, visible, score_scale):
    scores = (
        jnp.einsum("qhd,gkhd->qghk", query_heads, key_blocks, preferred_element_type=jnp.float32)
        * score_scale
    )
    visible_head = visible[:, :, None, :]
    masked = jnp.where(visible_head, scores, very_low)
    maxima = jnp.max(masked, axis=3)
    weights = jnp.exp(jnp.where(visible_head, scores - maxima[..., None], -jnp.inf))
    totals = jnp.sum(weights, axis=3)
    rounded = weights.astype(jnp.bfloat16)
    products = jnp.einsum(
        "qghk,gkhd->qghd", rounded, value_blocks, preferred_element_type=jnp.float32
    )
    return (maxima, totals, products)


def absorb(running, terms):
    largest, weight_sum, weighted = running
    maxima, totals, products = terms
    new_largest = jnp.maximum(largest, jnp.max(maxima, axis=1))
    old_factor = jnp.exp(largest - new_largest)
    factors = jnp.exp(maxima - new_largest[:, None, :])
    weight_sum = weight_sum * old_factor + jnp.sum(factors * totals, axis=1)
    weighted = weighted * old_factor[..., None] + jnp.sum(factors[..., None] * products, axis=1)
    return (new_largest, weight_sum, weighted)


def body(queries, slab_keys, slab_values, cache_keys, cache_values, offset, slab_len):
    device_rank = lax.axis_index("ctx")
    device_count = lax.axis_size("ctx")
    own_rows = queries.shape[0]
    slab_rows = own_rows * device_count
    cache_rows = cache_keys.shape[0]
    head_count = queries.shape[1] // DH
    score_scale = DH ** (-0.5)
    gathered = lax.all_gather(queries, "ctx", axis=0, tiled=True)
    query_heads = gathered.reshape(slab_rows, head_count, DH)
    running = (
        jnp.full((slab_rows, head_count), very_low, jnp.float32),
        jnp.zeros((slab_rows, head_count), jnp.float32),
        jnp.zeros((slab_rows, head_count, DH), jnp.float32),
    )
    for block_number in range(cache_rows // KB):
        block_start = block_number * KB
        key_blocks = cache_keys[block_start : block_start + KB].reshape(1, KB, head_count, DH)
        value_blocks = cache_values[block_start : block_start + KB].reshape(1, KB, head_count, DH)
        positions = device_rank * cache_rows + block_start + jnp.arange(KB, dtype=jnp.int32)
        visible = jnp.broadcast_to((positions < offset[0])[None, None, :], (slab_rows, 1, KB))
        running = absorb(
            running, block_state(query_heads, key_blocks, value_blocks, visible, score_scale)
        )
    own_index = device_rank * own_rows + jnp.arange(own_rows, dtype=jnp.int32)
    largest, weight_sum, weighted = running
    quotient = (weighted / jnp.maximum(weight_sum, 1.0)[..., None]).astype(jnp.bfloat16)
    parts_quotient = lax.all_to_all(
        quotient.reshape(1, slab_rows, head_count * DH),
        "ctx",
        split_axis=1,
        concat_axis=0,
        tiled=True,
    )
    parts_sum, parts_largest = (
        lax.all_to_all(weight_sum[None], "ctx", split_axis=1, concat_axis=0, tiled=True),
        lax.all_to_all(largest[None], "ctx", split_axis=1, concat_axis=0, tiled=True),
    )
    own_largest = jnp.max(parts_largest, axis=0)
    factors = jnp.exp(parts_largest - own_largest[None]) * parts_sum
    own_sum = jnp.sum(factors, axis=0)
    own_weighted = jnp.sum(
        factors[..., None]
        * parts_quotient.reshape(device_count, own_rows, head_count, DH).astype(jnp.float32),
        axis=0,
    )
    own_state = (own_largest, own_sum, own_weighted)
    own_queries = queries.reshape(own_rows, head_count, DH)
    keys_piece = lax.all_gather(slab_keys, "ctx", axis=0, tiled=True)
    values_piece = lax.all_gather(slab_values, "ctx", axis=0, tiled=True)
    piece_rows = keys_piece.shape[0]
    piece_blocks = piece_rows // own_rows
    key_index = jnp.arange(piece_rows, dtype=jnp.int32).reshape(piece_blocks, own_rows)
    visible = (key_index[None] <= own_index[:, None, None]) & (key_index[None] < slab_len[0])
    own_state = absorb(
        own_state,
        block_state(
            own_queries,
            keys_piece.reshape(piece_blocks, own_rows, head_count, DH),
            values_piece.reshape(piece_blocks, own_rows, head_count, DH),
            visible,
            score_scale,
        ),
    )
    final_largest, final_sum, final_weighted = own_state
    combined = (final_weighted / final_sum[..., None]).reshape(own_rows, head_count * DH)
    combined = jnp.where((own_index < slab_len[0])[:, None], combined, 0.0)
    return combined.astype(jnp.bfloat16)


def solution(mesh):
    placed = (
        P(("groups", "ctx"), None),
        P(("groups", "ctx"), None),
        P(("groups", "ctx"), None),
        P(("groups", "ctx"), None),
        P(("groups", "ctx"), None),
        P("groups"),
        P("groups"),
    )
    return jax.shard_map(
        body, mesh=mesh, in_specs=placed, out_specs=P(("groups", "ctx"), None), check_vma=False
    )
```

profile of v0, /device:TPU:0, one launch (start us, length us, event | category | flops | bytes accessed | tf_op | source)
XLA Modules:
  0.0 140.0 jit_solution(13504468689925622335)
XLA Ops:
  0.7 1.7 %fusion.59 = (bf16[256,2048]{1,0:T(8,128)(2,1)S(1)}, bf16[256,2048]{1,0:T(8,128)(2,1)S(1)}) fusion(bf16[512,2048]{1,0:T(8,128)(2,1)} %param.10), kind=kLoop, calls=%fused_computation.94 | loop fusion | bytes 4194304 | tf_op jit(solution)/shard_map/slice | solution.py:58
  2.3 0.5 copy.95
  2.9 0.2 copy-done.5
  3.1 24.6 %all_gather.9 = bf16[128,2048]{1,0:T(8,128)(2,1)S(1)} all-gather(bf16[8,2048]{1,0:T(8,128)(2,1)S(1)} %copy-done.5), channel_id=1, replica_groups=mesh['groups'=2,'ctx'=16] {'ctx'}, dimensions={0}, use_global_device_ids=true | all-gather | bytes 557056 | tf_op jit(solution)/shard_map/all_gather | solution.py:49
  27.7 0.3 copy.62
  28.0 1.3 copy.96
  29.3 0.6 fusion.3
  29.9 0.5 fusion.7
  30.5 0.6 fusion
  31.3 0.5 fusion.9
  31.9 0.5 broadcast.194
  32.3 0.7 reduce.7
  33.0 0.7 reshape.418
  33.7 3.5 %all-to-all-start = ((f32[16,1,128]{2,1,0:T(1,128)}), f32[16,1,128]{2,1,0:T(1,128)S(1)}, u32[]{:S(2)}, u32[]{:S(2)}) async-start(f32[16,1,128]{2,1,0:T(1,128)} %reshape.418), calls=%async_computation | async-start | bytes 16384 | tf_op jit(solution)/shard_map/all_to_all | solution.py:77
  37.9 23.2 %all_gather.10 = bf16[128,2048]{1,0:T(8,128)(2,1)S(1)} all-gather(bf16[8,2048]{1,0:T(8,128)(2,1)S(1)} %copy-done.4), channel_id=1, replica_groups=mesh['groups'=2,'ctx'=16] {'ctx'}, dimensions={0}, use_global_device_ids=true | all-gather | bytes 557056 | tf_op jit(solution)/shard_map/all_gather | solution.py:89
  61.2 0.9 copy.112
  62.1 3.1 %fusion.58 = (bf16[256,2048]{1,0:T(8,128)(2,1)}, bf16[256,2048]{1,0:T(8,128)(2,1)}) fusion(bf16[512,2048]{1,0:T(8,128)(2,1)} %param.11), kind=kLoop, calls=%fused_computation.93 | loop fusion | bytes 4194304 | tf_op jit(solution)/shard_map/slice | solution.py:59
  65.1 1.5 %copy.71 = bf16[256,2048]{0,1:T(8,128)(2,1)S(1)} copy(bf16[256,2048]{1,0:T(8,128)(2,1)} %get-tuple-element.16) | data formatting | bytes 2097152 | tf_op jit(solution)/shard_map/slice | solution.py:59
  66.6 3.3 %fusion.12 = f32[128,1,16,128]{0,3,2,1:T(8,128)} fusion(bf16[256,16,128]{0,2,1:T(8,128)(2,1)S(1)} %bitcast.143, f32[16,256,128]{2,1,0:T(8,128)} %copy-done, f32[128,16]{0,1:T(8,128)S(1)} %get-tuple-element.29, pred[256]{0:T(512)(128)(4,1)S(1)} %get-tuple-element.32, f32[128,16]{0,1:T(8,128)S(1)} %get-tuple-element.23), kind=kOutput, calls=%fused_computation.20 | convolution fusion | flops 136577024 | bytes 4210944 | tf_op jit(solution)/shard_map/qghk,gkhd->qghd/dot_general | solution.py:24
  69.9 3.6 %copy.73 = f32[1,128,2048]{2,0,1:T(1,128)} copy(f32[1,128,2048]{1,2,0:T(8,128)} %bitcast.144) | data formatting | bytes 2097152 | tf_op jit(solution)/shard_map/reduce_sum | solution.py:37
  73.6 1.5 %copy.75 = bf16[256,2048]{0,1:T(8,128)(2,1)S(1)} copy(bf16[256,2048]{1,0:T(8,128)(2,1)} %get-tuple-element.17) | data formatting | bytes 2097152 | tf_op jit(solution)/shard_map/slice | solution.py:59
  75.0 1.8 %fusion.13 = f32[128,1,16,128]{0,3,2,1:T(8,128)} fusion(bf16[256,16,128]{0,2,1:T(8,128)(2,1)S(1)} %bitcast.145, f32[16,256,128]{2,1,0:T(8,128)S(1)} %get-tuple-element.28, f32[128,16]{0,1:T(8,128)S(1)} %get-tuple-element.27, pred[256]{0:T(512)(128)(4,1)S(1)} %get-tuple-element.31, f32[128,16]{0,1:T(8,128)S(1)} %get-tuple-element.15), kind=kOutput, calls=%fused_computation.21 | convolution fusion | flops 136577024 | bytes 4210944 | tf_op jit(solution)/shard_map/qghk,gkhd->qghd/dot_general | solution.py:24
  76.8 2.5 %copy.77 = f32[1,128,2048]{2,0,1:T(1,128)S(1)} copy(f32[1,128,2048]{1,2,0:T(8,128)} %bitcast.146) | data formatting | bytes 2097152 | tf_op jit(solution)/shard_map/reduce_sum | solution.py:37
  79.8 0.5 select_reduce_fusion
  80.3 0.3 mul.193
  80.6 0.3 mul.197
  81.0 0.3 div.29
  81.3 0.2 copy-done.1
  81.5 3.3 %fusion.60 = bf16[128,1,2048]{2,1,0:T(2,128)(2,1)S(1)} fusion(f32[1,128,2048]{2,0,1:T(1,128)S(1)} %bitcast.152, f32[1,128,2048]{2,0,1:T(1,128)S(1)} %copy.77, f32[1,128,2048]{2,0,1:T(1,128)S(1)} %bitcast.151, f32[1,128,2048]{2,0,1:T(1,128)S(1)} %bitcast.150, f32[1,128,2048]{2,0,1:T(1,128)S(1)} %copy-done.1), kind=kLoop, calls=%fused_computation.96 | loop fusion | flops 1310720 | bytes 5767168
  84.8 0.6 fusion.28
  85.5 0.7 reduce.10
  86.2 0.7 reshape.422
  86.9 3.5 %all-to-all-start.1 = ((f32[16,1,128]{2,1,0:T(1,128)}), f32[16,1,128]{2,1,0:T(1,128)S(1)}, u32[]{:S(2)}, u32[]{:S(2)}) async-start(f32[16,1,128]{2,1,0:T(1,128)} %reshape.422), calls=%async_computation.1 | async-start | bytes 16384 | tf_op jit(solution)/shard_map/all_to_all | solution.py:76
  90.4 23.4 %all_gather.11 = bf16[128,2048]{1,0:T(8,128)(2,1)S(1)} all-gather(bf16[8,2048]{1,0:T(8,128)(2,1)S(1)} %copy-done.6), channel_id=1, replica_groups=mesh['groups'=2,'ctx'=16] {'ctx'}, dimensions={0}, use_global_device_ids=true | all-gather | bytes 557056 | tf_op jit(solution)/shard_map/all_gather | solution.py:90
  113.9 0.5 broadcast.196
  114.4 3.7 %reduce.9 = bf16[128,2048]{1,0:T(8,128)(2,1)S(1)} reduce(bf16[128,1,2048]{2,1,0:T(2,128)(2,1)S(1)} %fusion.60, bf16[]{:T(256)} %broadcast.196), dimensions={1}, to_apply=%fusion.60.reduce_sub_computation | reduce | bytes 1048578
  118.1 1.3 reshape.420
  119.4 3.6 %all-to-all-start.2 = ((bf16[16,2,8192]{2,1,0:T(2,128)(2,1)}), bf16[16,2,8192]{2,1,0:T(2,128)(2,1)S(1)}, u32[]{:S(2)}, u32[]{:S(2)}) async-start(bf16[16,2,8192]{2,1,0:T(2,128)(2,1)} %reshape.420), calls=%async_computation.2 | async-start | bytes 1048576 | tf_op jit(solution)/shard_map/all_to_all | solution.py:68
  123.0 0.6 reduce.8
  123.6 0.1 reshape.419
  123.8 0.6 reduce.11
  124.3 0.1 reshape.423
  124.8 0.6 fusion.14
  125.4 11.8 %all-to-all-done.2 = bf16[16,2,8192]{2,1,0:T(2,128)(2,1)S(1)} async-done(((bf16[16,2,8192]{2,1,0:T(2,128)(2,1)}), bf16[16,2,8192]{2,1,0:T(2,128)(2,1)S(1)}, u32[]{:S(2)}, u32[]{:S(2)}) %all-to-all-start.2) | async-done | bytes 524320 | tf_op jit(solution)/shard_map/all_to_all | solution.py:68
  137.3 0.5 reshape.421
  137.8 1.1 bitcast_convert_fusion
  138.9 0.4 multiply_reduce_fusion
  139.3 0.7 fusion.33
  (37 shorter events, 1.4 us)
Async XLA Ops:
  2.3 0.8 copy-start.5
  29.3 1.2 copy-start.2
  29.9 1.4 copy-start
  31.3 6.7 %copy-start.4 = (bf16[8,2048]{1,0:T(8,128)(2,1)S(1)}, bf16[8,2048]{1,0:T(8,128)(2,1)}, u32[]{:S(2)}) copy-start(bf16[8,2048]{1,0:T(8,128)(2,1)} %param.8) | copy-start | bytes 98308
  33.7 53.2 %all-to-all-start = ((f32[16,1,128]{2,1,0:T(1,128)}), f32[16,1,128]{2,1,0:T(1,128)S(1)}, u32[]{:S(2)}, u32[]{:S(2)}) async-start(f32[16,1,128]{2,1,0:T(1,128)} %reshape.418), calls=%async_computation | async-start | bytes 16384 | tf_op jit(solution)/shard_map/all_to_all | solution.py:77
  76.8 2.9 %copy-start.3 = (bf16[16,8,16,128]{3,2,1,0:T(8,128)(2,1)S(1)}, bf16[16,8,16,128]{3,2,1,0:T(8,128)(2,1)}, u32[]{:S(2)}) copy-start(bf16[16,8,16,128]{3,2,1,0:T(8,128)(2,1)} %copy.112) | copy-start | bytes 1572868
  80.3 1.2 copy-start.1
  84.8 5.6 %copy-start.6 = (bf16[8,2048]{1,0:T(8,128)(2,1)S(1)}, bf16[8,2048]{1,0:T(8,128)(2,1)}, u32[]{:S(2)}) copy-start(bf16[8,2048]{1,0:T(8,128)(2,1)} %param.9) | copy-start | bytes 98308
  86.9 32.5 %all-to-all-start.1 = ((f32[16,1,128]{2,1,0:T(1,128)}), f32[16,1,128]{2,1,0:T(1,128)S(1)}, u32[]{:S(2)}, u32[]{:S(2)}) async-start(f32[16,1,128]{2,1,0:T(1,128)} %reshape.422), calls=%async_computation.1 | async-start | bytes 16384 | tf_op jit(solution)/shard_map/all_to_all | solution.py:76
  119.4 17.8 %all-to-all-start.2 = ((bf16[16,2,8192]{2,1,0:T(2,128)(2,1)}), bf16[16,2,8192]{2,1,0:T(2,128)(2,1)S(1)}, u32[]{:S(2)}, u32[]{:S(2)}) async-start(bf16[16,2,8192]{2,1,0:T(2,128)(2,1)} %reshape.420), calls=%async_computation.2 | async-start | bytes 1048576 | tf_op jit(solution)/shard_map/all_to_all | solution.py:68
where the time goes:
time: 141 us; the launch traced here: 140 us
  blocking collectives  71.2 us (50%)
  local copies, waits for them, and re-layouts  23.8 us (17%)
  other arithmetic  13.6 us (10%)
  waiting for transfers between devices  11.9 us (8%)
  starting transfers between devices  10.5 us (7%)
  matrix products  7.41 us (5%)
  between operations  1.62 us (1%)
    all_gather x1, blocking collectives, body(): gathered = lax.all_gather(queries, 'ctx', axis=0, tiled=True)  24.6 us
    all_gather x1, blocking collectives, body(): values_piece = lax.all_gather(slab_values, 'ctx', axis=0, tiled=True)  23.4 us
    all_gather x1, blocking collectives, body(): keys_piece = lax.all_gather(slab_keys, 'ctx', axis=0, tiled=True)  23.2 us
    all_to_all x1, waiting for transfers between devices, body(): lax.all_to_all(quotient.reshape(1, slab_rows, head_count * DH), 'ctx', sp...  11.8 us
    unnamed x5, other arithmetic  8.48 us
    unnamed x25, local copies, waits for them, and re-layouts  7.98 us
    reduce_sum x2, local copies, waits for them, and re-layouts, absorb(): jnp.sum(factors[..., None] * products, axis=1)  6.12 us
    slice x3, local copies, waits for them, and re-layouts, body(): cache_values[block_start:block_start + KB].reshape(1, KB, head_count, DH)  6.04 us
  transfers between devices with their start and end apart: 3, of which 1 were waited for; matrix products, arithmetic and copies ran while one was open for 24% of the time, Pallas kernels for 0%

commit v1 on v0

v1 whole, which is shorter than its diff:
```python
import functools
import math

import jax
import jax.numpy as jnp
from jax import lax
from jax.experimental import pallas as pl
from jax.experimental.pallas import tpu as pltpu
from jax.sharding import PartitionSpec as P

DH = 128
LOWEST = -1e30
FLOOR = -1e29
EXP_SCALE = DH ** (-0.5) * math.log2(math.e)
GROUP_HEADS = 2


def kernel(
    n, offset_ref, slab_len_ref, q_ref, sk_ref, sv_ref, ck_ref, cv_ref, out_ref,
    qb, kb, vb, skb, svb, qs, sks, svs, ob, rb, sb, rs, fs, fr,
    local_sem, pair_send, pair_recv, q_send, q_recv, o_send, o_recv, s_send, s_recv,
):
    me = lax.axis_index("ctx")
    core = lax.rem(me, 2)
    other = 1 - core
    chip = lax.div(me, 2)
    chips = n // 2
    own_rows, width = q_ref.shape
    half = width // 2
    cache_rows = ck_ref.shape[0]
    chip_rows = 2 * own_rows
    slab_rows = n * own_rows
    heads = half // DH
    groups = heads // GROUP_HEADS
    mine = pl.ds(pl.multiple_of(core * half, half), half)
    theirs = pl.ds(pl.multiple_of(other * half, half), half)
    key_rows = pl.ds(pl.multiple_of(core * cache_rows, cache_rows), cache_rows)
    partner = {"ctx": chip * 2 + other}

    def peer(step):
        return {"ctx": lax.rem(chip + step, chips) * 2 + core}

    moves = (
        (q_ref, qb.at[chip, core]),
        (ck_ref, kb.at[key_rows]),
        (cv_ref, vb.at[key_rows]),
        (sk_ref, skb.at[core]),
        (sv_ref, svb.at[core]),
    )
    local = [
        pltpu.make_async_copy(src.at[:, mine], dst, local_sem.at[i])
        for i, (src, dst) in enumerate(moves)
    ]
    for copy in local:
        copy.start()

    barrier = pltpu.get_barrier_semaphore()
    pl.semaphore_signal(barrier, inc=1, device_id=partner, device_id_type=pl.DeviceIdType.MESH)
    for step in range(1, chips):
        pl.semaphore_signal(
            barrier, inc=1, device_id=peer(step), device_id_type=pl.DeviceIdType.MESH
        )
    pl.semaphore_wait(barrier, chips)

    pair = [
        pltpu.make_async_remote_copy(
            src_ref=src.at[:, theirs], dst_ref=dst,
            send_sem=pair_send.at[i], recv_sem=pair_recv.at[i],
            device_id=partner, device_id_type=pl.DeviceIdType.MESH,
        )
        for i, (src, dst) in enumerate(moves)
    ]
    for copy in pair:
        copy.start()

    def send(src, dst, send_sem, recv_sem, device):
        copy = pltpu.make_async_remote_copy(
            src_ref=src, dst_ref=dst, send_sem=send_sem, recv_sem=recv_sem,
            device_id=device, device_id_type=pl.DeviceIdType.MESH,
        )
        copy.start()
        return copy

    local[0].wait()
    pair[0].wait()
    q_copies = [
        send(qb.at[chip], qb.at[chip], q_send.at[step], q_recv.at[step], peer(step))
        for step in range(1, chips)
    ]
    for copy in local[1:] + pair[1:]:
        copy.wait()
    sks[...] = skb[...].astype(jnp.float32).reshape(chip_rows, half).astype(jnp.bfloat16)
    svs[...] = svb[...].astype(jnp.float32).reshape(chip_rows, half).astype(jnp.bfloat16)
    offset = offset_ref[0]
    slab_len = slab_len_ref[0]
    position = chip * (2 * cache_rows) + lax.broadcasted_iota(jnp.int32, (1, 2 * cache_rows), 1)
    cache_bias = jnp.where(position < offset, 0.0, LOWEST)
    row = lax.broadcasted_iota(jnp.int32, (slab_rows, chip_rows), 0)
    column = chip * chip_rows + lax.broadcasted_iota(jnp.int32, (slab_rows, chip_rows), 1)
    slab_bias = jnp.where((column <= row) & (column < slab_len), 0.0, LOWEST)
    lane = lax.broadcasted_iota(jnp.int32, (slab_rows, DH), 1)

    for copy in q_copies:
        copy.wait()
    qs[...] = qb[...].astype(jnp.float32).reshape(slab_rows, half).astype(jnp.bfloat16)

    across = (((1,), (1,)), ((), ()))
    stats = jnp.zeros((slab_rows, DH), jnp.float32)
    o_copies = []
    for group in range(groups):
        for inner in range(GROUP_HEADS):
            h = group * GROUP_HEADS + inner
            cols = slice(h * DH, (h + 1) * DH)
            q = qs[:, cols]
            scores = lax.dot_general(
                q, kb[:, cols], across, preferred_element_type=jnp.float32
            ) + cache_bias
            slab_scores = lax.dot_general(
                q, sks[:, cols], across, preferred_element_type=jnp.float32
            ) + slab_bias
            largest = jnp.maximum(
                jnp.max(scores, axis=1, keepdims=True),
                jnp.max(slab_scores, axis=1, keepdims=True),
            )
            largest = jnp.maximum(largest, FLOOR)
            weights = jnp.exp2((scores - largest) * EXP_SCALE)
            slab_weights = jnp.exp2((slab_scores - largest) * EXP_SCALE)
            total = jnp.sum(weights, axis=1, keepdims=True) + jnp.sum(
                slab_weights, axis=1, keepdims=True
            )
            summed = jnp.dot(
                weights.astype(jnp.bfloat16), vb[:, cols], preferred_element_type=jnp.float32
            ) + jnp.dot(
                slab_weights.astype(jnp.bfloat16), svs[:, cols],
                preferred_element_type=jnp.float32,
            )
            stats = jnp.where(lane == h, largest, stats)
            stats = jnp.where(lane == heads + h, total, stats)
            ob[group, :, :, inner * DH : (inner + 1) * DH] = summed.reshape(
                chips, chip_rows, DH
            ).astype(jnp.bfloat16)
        for step in range(1, chips):
            target = lax.rem(chip + step, chips)
            o_copies.append(
                send(
                    ob.at[group, target], rb.at[group, step],
                    o_send.at[group, step], o_recv.at[group, step], peer(step),
                )
            )
    sb[...] = stats.reshape(chips, chip_rows, DH)
    s_copies = []
    for step in range(1, chips):
        target = lax.rem(chip + step, chips)
        s_copies.append(
            send(sb.at[target], rs.at[step], s_send.at[step], s_recv.at[step], peer(step))
        )
    for copy in s_copies:
        copy.wait()
    parts = [sb[chip]] + [rs[step] for step in range(1, chips)]
    top = functools.reduce(jnp.maximum, parts)
    factors = [jnp.exp2(jnp.minimum(part - top, 0.0) * EXP_SCALE) for part in parts]
    denominator = sum(
        factor * pltpu.roll(part, DH - heads, 1) for factor, part in zip(factors, parts)
    )
    inverse = 1.0 / denominator
    shares = [factor * inverse for factor in factors]
    out_row = chip * chip_rows + lax.broadcasted_iota(jnp.int32, (chip_rows, DH), 0)
    valid = out_row < slab_len
    for copy in o_copies:
        copy.wait()
    for h in range(heads):
        group, inner = divmod(h, GROUP_HEADS)
        cols = slice(inner * DH, (inner + 1) * DH)
        mixed = shares[0][:, h : h + 1] * ob[group, chip, :, cols].astype(jnp.float32)
        for step in range(1, chips):
            mixed = mixed + shares[step][:, h : h + 1] * rb[group, step, :, cols].astype(
                jnp.float32
            )
        mixed = jnp.where(valid, mixed, 0.0)
        fs[:, :, h * DH : (h + 1) * DH] = mixed.reshape(2, own_rows, DH).astype(jnp.bfloat16)
    last = send(
        fs.at[other], fr, pair_send.at[len(moves)], pair_recv.at[len(moves)], partner
    )
    out_ref[:, mine] = fs[core]
    last.wait()
    out_ref[:, theirs] = fr[...]


def body(queries, slab_keys, slab_values, cache_keys, cache_values, offset, slab_len):
    n = lax.axis_size("ctx")
    own_rows, width = queries.shape
    cache_rows = cache_keys.shape[0]
    chips, half, chip_rows = n // 2, width // 2, 2 * own_rows
    groups = half // DH // GROUP_HEADS
    wide = GROUP_HEADS * DH
    bf16, f32 = jnp.bfloat16, jnp.float32
    dma = pltpu.SemaphoreType.DMA
    vmem = pl.BlockSpec(memory_space=pltpu.VMEM)
    smem = pl.BlockSpec(memory_space=pltpu.SMEM)
    hbm = pl.BlockSpec(memory_space=pl.ANY)
    return pl.pallas_call(
        functools.partial(kernel, n),
        out_shape=jax.ShapeDtypeStruct(queries.shape, queries.dtype),
        in_specs=[smem, smem, vmem, vmem, vmem, hbm, hbm],
        out_specs=vmem,
        scratch_shapes=[
            pltpu.VMEM((chips, 2, own_rows, half), bf16),
            pltpu.VMEM((2 * cache_rows, half), bf16),
            pltpu.VMEM((2 * cache_rows, half), bf16),
            pltpu.VMEM((2, own_rows, half), bf16),
            pltpu.VMEM((2, own_rows, half), bf16),
            pltpu.VMEM((n * own_rows, half), bf16),
            pltpu.VMEM((chip_rows, half), bf16),
            pltpu.VMEM((chip_rows, half), bf16),
            pltpu.VMEM((groups, chips, chip_rows, wide), bf16),
            pltpu.VMEM((groups, chips, chip_rows, wide), bf16),
            pltpu.VMEM((chips, chip_rows, DH), f32),
            pltpu.VMEM((chips, chip_rows, DH), f32),
            pltpu.VMEM((2, own_rows, half), bf16),
            pltpu.VMEM((own_rows, half), bf16),
            dma((5,)),
            dma((6,)),
            dma((6,)),
            dma((chips,)),
            dma((chips,)),
            dma((groups, chips)),
            dma((groups, chips)),
            dma((chips,)),
            dma((chips,)),
        ],
        compiler_params=pltpu.CompilerParams(collective_id=0, has_side_effects=True),
    )(offset, slab_len, queries, slab_keys, slab_values, cache_keys, cache_values)


def solution(mesh):
    rows = P(("groups", "ctx"), None)
    placed = (rows, rows, rows, rows, rows, P("groups"), P("groups"))
    return jax.shard_map(
        body, mesh=mesh, in_specs=placed, out_specs=rows, check_vma=False
    )
```

time: 141 us -> 31 us (0.22)
  blocking collectives: 71.2 us -> 0 us
  Pallas kernels: 0 us -> 28.1 us
  local copies, waits for them, and re-layouts: 23.8 us -> 1.38 us
  other arithmetic: 13.6 us -> 0 us
  waiting for transfers between devices: 11.9 us -> 0 us
  starting transfers between devices: 10.5 us -> 0 us
  matrix products: 7.41 us -> 0 us
    all_gather x3 -> x0, blocking collectives: 71.2 us -> none  [the longest x1 24.6 us: body(): gathered = lax.all_gather(queries, 'ctx', axis=0, tiled=True)]
    pallas_call x0 -> x1, Pallas kernels: none -> 28.1 us  [body(): pl.pallas_call(functools.partial(kernel, n), out_shape=jax.ShapeDtypeStru...]
    all_to_all x3 -> x0, waiting for transfers between devices: 11.9 us -> none  [the longest x1 11.8 us: body(): lax.all_to_all(quotient.reshape(1, slab_rows, head_count * DH), 'ctx', sp...]
    all_to_all x3 -> x0, starting transfers between devices: 10.5 us -> none  [the longest x1 3.57 us: body(): lax.all_to_all(quotient.reshape(1, slab_rows, head_count * DH), 'ctx', sp...]
    unnamed x5 -> x0, other arithmetic: 8.48 us -> none
    slice x4 -> x0, local copies, waits for them, and re-layouts: 7.71 us -> none  [the longest x3 6.04 us: body(): cache_values[block_start:block_start + KB].reshape(1, KB, head_count, DH)]
    dot_general x6 -> x0, matrix products: 7.41 us -> none  [the longest x3 5.69 us: block_state(): jnp.einsum('qghk,gkhd->qghd', rounded, value_blocks, preferred_element_ty...]
    unnamed x25 -> x1, local copies, waits for them, and re-layouts: 7.98 us -> 1.38 us
  transfers between devices with their start and end apart: 3 -> 0, of which waited for: 1 -> 0; matrix products, arithmetic and copies ran while one was open for 24% -> 0% of each run, Pallas kernels for 0% -> 0%
where the time goes in v1:
time: 31 us; the launch traced here: 30.7 us
  Pallas kernels  28.1 us (91%)
  local copies, waits for them, and re-layouts  1.38 us (4%)
  between operations  1.3 us (4%)
    pallas_call x1, Pallas kernels, body(): pl.pallas_call(functools.partial(kernel, n), out_shape=jax.ShapeDtypeStru...  28.1 us
    unnamed x1, local copies, waits for them, and re-layouts  1.38 us

profile of v1, /device:TPU:0, one launch (start us, length us, event | category | flops | bytes accessed | tf_op | source)
XLA Modules:
  0.0 30.7 jit_solution(8355257804762966095)
XLA Ops:
  1.3 28.1 %shard_map.73 = bf16[8,2048]{1,0:T(8,128)(2,1)} custom-call(s32[1]{0:T(128)S(6)} %copy.9.offset_ref, s32[1]{0:T(128)S(6)} %copy.10.slab_len_ref, bf16[8,2048]{1,0:T(8,128)(2,1)} %q_ref.1, bf16[8,2048]{1,0:T(8,128)(2,1)} %sk_ref.1, bf16[8,2048]{1,0:T(8,128)(2,1)} %sv_ref.1, bf16[512,2048]{1,0:T(8,128)(2,1)} %ck_ref.1, bf16[512,2048]{1,0:T(8,128)(2,1)} %cv_ref.1), custom_call_target="tpu_custom_call" | custom-call | tf_op jit(solution)/shard_map/pallas_call | solution.py:201
  29.4 1.4 %copy.11 = bf16[8,2048]{1,0:T(8,128)(2,1)} copy(bf16[8,2048]{1,0:T(8,128)(2,1)} %shard_map.73) | data formatting | bytes 65536

commit v2 on v1

--- a/solution.py
+++ b/solution.py
@@ -40,13 +40,24 @@
     def peer(step):
         return {"ctx": lax.rem(chip + step, chips) * 2 + core}
 
+    wide = GROUP_HEADS * DH
+
+    def part(base, group):
+        return pl.ds(pl.multiple_of(base * half + group * wide, wide), wide)
+
+    q_moves = [(q_ref, qb.at[group, chip, core], group) for group in range(groups)]
     moves = (
-        (q_ref, qb.at[chip, core]),
         (ck_ref, kb.at[key_rows]),
         (cv_ref, vb.at[key_rows]),
         (sk_ref, skb.at[core]),
         (sv_ref, svb.at[core]),
     )
+    q_local = [
+        pltpu.make_async_copy(src.at[:, part(core, group)], dst, local_sem.at[len(moves) + group])
+        for src, dst, group in q_moves
+    ]
+    for copy in q_local:
+        copy.start()
     local = [
         pltpu.make_async_copy(src.at[:, mine], dst, local_sem.at[i])
         for i, (src, dst) in enumerate(moves)
@@ -62,6 +73,21 @@
         )
     pl.semaphore_wait(barrier, chips)
 
+    def send(src, dst, send_sem, recv_sem, device):
+        copy = pltpu.make_async_remote_copy(
+            src_ref=src, dst_ref=dst, send_sem=send_sem, recv_sem=recv_sem,
+            device_id=device, device_id_type=pl.DeviceIdType.MESH,
+        )
+        copy.start()
+        return copy
+
+    q_pair = [
+        send(
+            src.at[:, part(other, group)], dst,
+            pair_send.at[len(moves) + group], pair_recv.at[len(moves) + group], partner,
+        )
+        for src, dst, group in q_moves
+    ]
     pair = [
         pltpu.make_async_remote_copy(
             src_ref=src.at[:, theirs], dst_ref=dst,
@@ -73,21 +99,20 @@
     for copy in pair:
         copy.start()
 
-    def send(src, dst, send_sem, recv_sem, device):
-        copy = pltpu.make_async_remote_copy(
-            src_ref=src, dst_ref=dst, send_sem=send_sem, recv_sem=recv_sem,
-            device_id=device, device_id_type=pl.DeviceIdType.MESH,
-        )
-        copy.start()
-        return copy
-
-    local[0].wait()
-    pair[0].wait()
-    q_copies = [
-        send(qb.at[chip], qb.at[chip], q_send.at[step], q_recv.at[step], peer(step))
-        for step in range(1, chips)
-    ]
-    for copy in local[1:] + pair[1:]:
+    q_copies = []
+    for group in range(groups):
+        q_local[group].wait()
+        q_pair[group].wait()
+        q_copies.append(
+            [
+                send(
+                    qb.at[group, chip], qb.at[group, chip],
+                    q_send.at[group, step], q_recv.at[group, step], peer(step),
+                )
+                for step in range(1, chips)
+            ]
+        )
+    for copy in local + pair:
         copy.wait()
     sks[...] = skb[...].astype(jnp.float32).reshape(chip_rows, half).astype(jnp.bfloat16)
     svs[...] = svb[...].astype(jnp.float32).reshape(chip_rows, half).astype(jnp.bfloat16)
@@ -100,18 +125,17 @@
     slab_bias = jnp.where((column <= row) & (column < slab_len), 0.0, LOWEST)
     lane = lax.broadcasted_iota(jnp.int32, (slab_rows, DH), 1)
 
-    for copy in q_copies:
-        copy.wait()
-    qs[...] = qb[...].astype(jnp.float32).reshape(slab_rows, half).astype(jnp.bfloat16)
-
     across = (((1,), (1,)), ((), ()))
     stats = jnp.zeros((slab_rows, DH), jnp.float32)
     o_copies = []
     for group in range(groups):
+        for copy in q_copies[group]:
+            copy.wait()
+        qs[...] = qb[group].astype(jnp.float32).reshape(slab_rows, wide).astype(jnp.bfloat16)
         for inner in range(GROUP_HEADS):
             h = group * GROUP_HEADS + inner
             cols = slice(h * DH, (h + 1) * DH)
-            q = qs[:, cols]
+            q = qs[:, inner * DH : (inner + 1) * DH]
             scores = lax.dot_general(
                 q, kb[:, cols], across, preferred_element_type=jnp.float32
             ) + cache_bias
@@ -147,7 +171,9 @@
                     o_send.at[group, step], o_recv.at[group, step], peer(step),
                 )
             )
-    sb[...] = stats.reshape(chips, chip_rows, DH)
+    stats = stats.reshape(chips, 2, own_rows, DH)
+    low = lax.broadcasted_iota(jnp.int32, (chips, own_rows, DH), 2) < DH // 2
+    sb[...] = jnp.where(low, stats[:, 0], pltpu.roll(stats[:, 1], DH // 2, 2))
     s_copies = []
     for step in range(1, chips):
         target = lax.rem(chip + step, chips)
@@ -164,6 +190,9 @@
     )
     inverse = 1.0 / denominator
     shares = [factor * inverse for factor in factors]
+    shares = [
+        jnp.concatenate([share, pltpu.roll(share, DH // 2, 1)], axis=0) for share in shares
+    ]
     out_row = chip * chip_rows + lax.broadcasted_iota(jnp.int32, (chip_rows, DH), 0)
     valid = out_row < slab_len
     for copy in o_copies:
@@ -179,7 +208,7 @@
         mixed = jnp.where(valid, mixed, 0.0)
         fs[:, :, h * DH : (h + 1) * DH] = mixed.reshape(2, own_rows, DH).astype(jnp.bfloat16)
     last = send(
-        fs.at[other], fr, pair_send.at[len(moves)], pair_recv.at[len(moves)], partner
+        fs.at[other], fr, pair_send.at[len(moves) + groups], pair_recv.at[len(moves) + groups], partner
     )
     out_ref[:, mine] = fs[core]
     last.wait()
@@ -204,25 +233,25 @@
         in_specs=[smem, smem, vmem, vmem, vmem, hbm, hbm],
         out_specs=vmem,
         scratch_shapes=[
-            pltpu.VMEM((chips, 2, own_rows, half), bf16),
+            pltpu.VMEM((groups, chips, 2, own_rows, wide), bf16),
             pltpu.VMEM((2 * cache_rows, half), bf16),
             pltpu.VMEM((2 * cache_rows, half), bf16),
             pltpu.VMEM((2, own_rows, half), bf16),
             pltpu.VMEM((2, own_rows, half), bf16),
-            pltpu.VMEM((n * own_rows, half), bf16),
+            pltpu.VMEM((n * own_rows, wide), bf16),
             pltpu.VMEM((chip_rows, half), bf16),
             pltpu.VMEM((chip_rows, half), bf16),
             pltpu.VMEM((groups, chips, chip_rows, wide), bf16),
             pltpu.VMEM((groups, chips, chip_rows, wide), bf16),
-            pltpu.VMEM((chips, chip_rows, DH), f32),
-            pltpu.VMEM((chips, chip_rows, DH), f32),
+            pltpu.VMEM((chips, own_rows, DH), f32),
+            pltpu.VMEM((chips, own_rows, DH), f32),
             pltpu.VMEM((2, own_rows, half), bf16),
             pltpu.VMEM((own_rows, half), bf16),
-            dma((5,)),
-            dma((6,)),
-            dma((6,)),
-            dma((chips,)),
-            dma((chips,)),
+            dma((4 + groups,)),
+            dma((5 + groups,)),
+            dma((5 + groups,)),
+            dma((groups, chips)),
+            dma((groups, chips)),
             dma((groups, chips)),
             dma((groups, chips)),
             dma((chips,)),

time: 31 us -> 29.3 us (0.945)
  Pallas kernels: 28.1 us -> 26.3 us
    pallas_call x1, Pallas kernels: 28.1 us -> 26.3 us  [body(): pl.pallas_call(functools.partial(kernel, n), out_shape=jax.ShapeDtypeStru...]
where the time goes in v2:
time: 29.3 us; the launch traced here: 29 us
  Pallas kernels  26.3 us (90%)
  local copies, waits for them, and re-layouts  1.38 us (5%)
  between operations  1.3 us (4%)
    pallas_call x1, Pallas kernels, body(): pl.pallas_call(functools.partial(kernel, n), out_shape=jax.ShapeDtypeStru...  26.3 us
    unnamed x1, local copies, waits for them, and re-layouts  1.38 us

profile of v2, /device:TPU:0, one launch (start us, length us, event | category | flops | bytes accessed | tf_op | source)
XLA Modules:
  0.0 29.0 jit_solution(9332337083127350754)
XLA Ops:
  1.3 26.3 %shard_map.73 = bf16[8,2048]{1,0:T(8,128)(2,1)} custom-call(s32[1]{0:T(128)S(6)} %copy.9.offset_ref, s32[1]{0:T(128)S(6)} %copy.10.slab_len_ref, bf16[8,2048]{1,0:T(8,128)(2,1)} %q_ref.1, bf16[8,2048]{1,0:T(8,128)(2,1)} %sk_ref.1, bf16[8,2048]{1,0:T(8,128)(2,1)} %sv_ref.1, bf16[512,2048]{1,0:T(8,128)(2,1)} %ck_ref.1, bf16[512,2048]{1,0:T(8,128)(2,1)} %cv_ref.1), custom_call_target="tpu_custom_call" | custom-call | tf_op jit(solution)/shard_map/pallas_call | solution.py:230
  27.6 1.4 %copy.11 = bf16[8,2048]{1,0:T(8,128)(2,1)} copy(bf16[8,2048]{1,0:T(8,128)(2,1)} %shard_map.73) | data formatting | bytes 65536
